TPU v7x, 32 devices: a whole 2x2x4 slice. The times are simulated.
32 devices in a mesh: dp: 2 (over y), expert: 16 (over z, x, core).
Axes of the slice: x: 2, y: 2, z: 4, core: 2. Of those that a mesh axis runs over, the one named last changes fastest.
Arguments:
- tokens: bfloat16 [512, 4096], P(('dp', 'expert')), may hold values from -6 to 6
- routing: int32 [512, 2], P(('dp', 'expert')), may hold values from 0 to 7, as said below
- hidden_grad: bfloat16 [2048, 4096], P(('dp', 'expert')), may hold values from -3 to 3
- gate_weight: bfloat16 [4096, 65536], P(None, 'expert'), may hold values from -0.09375 to 0.09375
- up_weight: bfloat16 [4096, 65536], P(None, 'expert'), may hold values from -0.09375 to 0.09375
Outputs:
- token_grad: bfloat16 [512, 4096], P(('dp', 'expert'))
- gate_weight_grad: bfloat16 [4096, 65536], P('dp', 'expert')
- up_weight_grad: bfloat16 [4096, 65536], P('dp', 'expert')
Inputs may be any that keep to these rules, and one draw needn't show every extreme that they name: `routing`: the 2 entries of a token differ, and no device names one expert in more than 4 of its tokens.
All inputs are finite; a program needn't handle non-finite values.
Results may differ from a plain program's by a relative error of at most 0.0085.
Values may be sent and summed in bfloat16 or wider, within the bound.
A program may use at most 256 MiB of HBM per device.

v0:
```python
import jax
import jax.numpy as jnp
from jax import lax
from jax.sharding import PartitionSpec as P

EXPERTS = 8
TOP = 2
CAP = 4


def from_partner(block, axis, apart):
    count = lax.axis_size(axis)
    route = []
    for low in range(count):
        high = low | 1 << apart
        if high != low and high < count:
            route += [(low, high), (high, low)]
    return lax.ppermute(block, axis, route)


def slot_tables(routing_dev):
    flat_experts = routing_dev.reshape(-1)
    onehot = (flat_experts[:, None] == jnp.arange(EXPERTS, dtype=jnp.int32)[None, :]).astype(
        jnp.int32
    )
    before = jnp.cumsum(onehot, axis=0) - onehot
    slot_index = jnp.sum(before * onehot, axis=1)
    target = flat_experts * CAP + slot_index
    placed = target[:, None] == jnp.arange(EXPERTS * CAP, dtype=jnp.int32)[None, :]
    return placed.astype(jnp.float32)


def contract_rows(left_rows, right_rows):
    return lax.dot_general(
        left_rows, right_rows, (((0,), (0,)), ((), ())), preferred_element_type=jnp.float32
    )


def rounded(value):
    return lax.optimization_barrier(value.astype(jnp.bfloat16)).astype(jnp.float32)


def per_device(tokens, routing, hidden_grad, gate_weight, up_weight):
    token_count = tokens.shape[0]
    model_width = tokens.shape[1]
    ffd_cols = gate_weight.shape[1]
    shards = lax.axis_size("expert") // EXPERTS
    placed = slot_tables(routing)
    doubled = jnp.repeat(tokens, TOP, axis=0)
    outgoing = jnp.dot(
        placed.T.astype(jnp.bfloat16), doubled, preferred_element_type=jnp.float32
    ).astype(jnp.bfloat16)
    copies = jnp.broadcast_to(
        outgoing.reshape(EXPERTS, 1, CAP, model_width), (EXPERTS, shards, CAP, model_width)
    )
    copies = copies.reshape(EXPERTS * shards, CAP, model_width)
    arrived = lax.all_to_all(copies, "expert", split_axis=0, concat_axis=0, tiled=True)
    expert_rows = arrived.reshape(-1, model_width)
    gate_pre = jnp.dot(expert_rows, gate_weight, preferred_element_type=jnp.float32)
    up_pre = jnp.dot(expert_rows, up_weight, preferred_element_type=jnp.float32)
    grad_h = hidden_grad.astype(jnp.float32)
    sigmoid_gate = jax.nn.sigmoid(gate_pre)
    gate_grad = (grad_h * up_pre * sigmoid_gate * (1.0 + gate_pre * (1.0 - sigmoid_gate))).astype(
        jnp.bfloat16
    )
    up_grad = (grad_h * gate_pre * sigmoid_gate).astype(jnp.bfloat16)
    transposed = (((1,), (1,)), ((), ()))
    partial_value = lax.dot_general(
        gate_grad, gate_weight, transposed, preferred_element_type=jnp.float32
    )
    partial_value = partial_value + lax.dot_general(
        up_grad, up_weight, transposed, preferred_element_type=jnp.float32
    )
    partial_value = partial_value.astype(jnp.bfloat16)
    returned = lax.all_to_all(
        partial_value.reshape(-1, CAP, model_width),
        "expert",
        split_axis=0,
        concat_axis=0,
        tiled=True,
    )
    summed = jnp.sum(
        returned.astype(jnp.float32).reshape(EXPERTS, shards, CAP, model_width), axis=1
    )
    summed = summed.reshape(EXPERTS * CAP, model_width)
    gathered = jnp.dot(placed, summed, precision=lax.Precision.HIGHEST)
    token_grad = jnp.sum(gathered.reshape(token_count, TOP, model_width), axis=1).astype(
        jnp.bfloat16
    )
    grads_pair = jnp.concatenate([gate_grad, up_grad], axis=1)
    half_width = model_width // lax.axis_size("dp")
    replica_index = lax.axis_index("dp")
    own_columns = lax.dynamic_slice_in_dim(expert_rows, replica_index * half_width, half_width, 1)
    far_columns = lax.dynamic_slice_in_dim(
        expert_rows, (1 - replica_index) * half_width, half_width, 1
    )
    their_columns = from_partner(far_columns, "dp", 0)
    their_grads = from_partner(grads_pair, "dp", 0)
    weight_sum = rounded(contract_rows(own_columns, grads_pair)) + rounded(
        contract_rows(their_columns, their_grads)
    )
    gate_weight_grad = weight_sum[:, :ffd_cols].astype(jnp.bfloat16)
    up_weight_grad = weight_sum[:, ffd_cols:].astype(jnp.bfloat16)
    return (token_grad, gate_weight_grad, up_weight_grad)


def solution(mesh):
    in_specs = (
        P(("dp", "expert"), None),
        P(("dp", "expert"), None),
        P(("dp", "expert"), None),
        P(None, "expert"),
        P(None, "expert"),
    )
    out_specs = (P(("dp", "expert"), None), P("dp", "expert"), P("dp", "expert"))
    return jax.shard_map(
        per_device, mesh=mesh, in_specs=in_specs, out_specs=out_specs, check_vma=False
    )
```

profile of v0, /device:TPU:0, one launch (start us, length us, event | category | flops | bytes accessed | tf_op | source)
XLA Modules:
  0.0 189.2 jit_solution(2620720750499844734)
XLA Ops:
  0.6 0.8 copy.16
  1.9 1.1 broadcast_in_dim.6
  3.1 0.2 convolution_convert_fusion.2
  3.4 1.0 broadcast_in_dim.15
  4.4 7.4 %all-to-all-start = ((bf16[16,4,4096]{2,1,0:T(4,128)(2,1)}), bf16[16,4,4096]{2,1,0:T(4,128)(2,1)S(1)}, u32[]{:S(2)}, u32[]{:S(2)}) async-start(bf16[16,4,4096]{2,1,0:T(4,128)(2,1)} %bitcast.1), calls=%async_computation | async-start | bytes 1048576 | tf_op jit(solution)/shard_map/all_to_all | solution.py:57
  12.0 0.7 multiply_add_fusion
  12.7 13.4 %all-to-all-done = bf16[16,4,4096]{2,1,0:T(4,128)(2,1)S(1)} async-done(((bf16[16,4,4096]{2,1,0:T(4,128)(2,1)}), bf16[16,4,4096]{2,1,0:T(4,128)(2,1)S(1)}, u32[]{:S(2)}, u32[]{:S(2)}) %all-to-all-start) | async-done | bytes 524320 | tf_op jit(solution)/shard_map/all_to_all | solution.py:57
  26.2 0.7 constant_dynamic-slice_fusion
  26.9 1.5 collective-permute-start
  28.4 14.0 %fusion.5 = (bf16[64,4096]{1,0:T(8,128)(2,1)S(1)}, f32[64,4096]{1,0:T(8,128)S(1)}) fusion(bf16[64,4096]{1,0:T(8,128)(2,1)} %param.7, bf16[64,4096]{1,0:T(8,128)(2,1)S(1)} %reshape.66, bf16[4096,4096]{1,0:T(8,128)(2,1)} %param.8), kind=kOutput, calls=%fused_computation.13 | convolution fusion | flops 2149318656 | bytes 36175872 | tf_op jit(solution)/shard_map/dot_general | solution.py:59
  42.5 14.0 %fusion.3 = bf16[64,4096]{1,0:T(8,128)(2,1)S(1)} fusion(bf16[64,4096]{1,0:T(8,128)(2,1)S(1)} %reshape.66, bf16[4096,4096]{1,0:T(8,128)(2,1)} %param.9, bf16[64,4096]{1,0:T(8,128)(2,1)S(1)} %copy-done, f32[64,4096]{1,0:T(8,128)S(1)} %get-tuple-element.6), kind=kOutput, calls=%fused_computation.8 | convolution fusion | flops 2150367232 | bytes 36175872 | tf_op jit(solution)/shard_map/dot_general | solution.py:60
  56.5 15.5 %fusion.14 = f32[64,4096]{1,0:T(8,128)S(1)} fusion(bf16[64,4096]{1,0:T(8,128)(2,1)S(1)} %fusion.3, bf16[4096,4096]{1,0:T(8,128)(2,1)} %param.8), kind=kOutput, calls=%fused_computation.32 | convolution fusion | flops 2147483648 | bytes 35127296 | tf_op jit(solution)/shard_map/dot_general | solution.py:68
  72.1 1.0 pad_maximum_fusion
  73.1 15.6 %fusion.2 = bf16[64,4096]{1,0:T(8,128)(2,1)S(1)} fusion(f32[64,4096]{1,0:T(8,128)S(1)} %fusion.14, bf16[64,4096]{1,0:T(8,128)(2,1)S(1)} %get-tuple-element.5, bf16[4096,4096]{1,0:T(8,128)(2,1)} %param.9), kind=kOutput, calls=%fused_computation.7 | convolution fusion | flops 2148007936 | bytes 35651584 | tf_op jit(solution)/shard_map/dot_general | solution.py:71
  88.7 1.0 reshape.67
  89.7 4.2 %all-to-all-start.1 = ((bf16[16,4,4096]{2,1,0:T(4,128)(2,1)}), bf16[16,4,4096]{2,1,0:T(4,128)(2,1)S(1)}, u32[]{:S(2)}, u32[]{:S(2)}) async-start(bf16[16,4,4096]{2,1,0:T(4,128)(2,1)} %reshape.67), calls=%async_computation.1 | async-start | bytes 1048576 | tf_op jit(solution)/shard_map/all_to_all | solution.py:75
  93.9 0.6 collective-permute-start.1
  94.5 13.6 %convolution_convert_fusion.1 = bf16[2048,8192]{1,0:T(8,128)(2,1)} fusion(bf16[64,4096]{1,0:T(8,128)(2,1)S(1)} %reshape.66, s32[]{:T(128)S(6)} %select_n.6, bf16[64,4096]{1,0:T(8,128)(2,1)S(1)} %get-tuple-element.5, bf16[64,4096]{1,0:T(8,128)(2,1)S(1)} %fusion.3), kind=kOutput, calls=%fused_computation.2 | convolution fusion | flops 2166358016 | bytes 34865156 | tf_op jit(solution)/shard_map/dot_general | solution.py:34
  108.2 0.3 convert_reduce_fusion
  108.6 1.1 convolution_reduce_fusion
  109.8 9.9 %collective-permute-done.1 = bf16[64,8192]{1,0:T(8,128)(2,1)S(1)} collective-permute-done((bf16[64,8192]{1,0:T(8,128)(2,1)}, bf16[64,8192]{1,0:T(8,128)(2,1)S(1)}, u32[]{:S(2)}, u32[]{:S(2)}) %collective-permute-start.1) | collective-permute-done | bytes 1048608 | tf_op jit(solution)/shard_map/ppermute | solution.py:18
  119.6 13.6 %convolution_convert_fusion = bf16[2048,8192]{1,0:T(8,128)(2,1)} fusion(bf16[64,2048]{1,0:T(8,128)(2,1)S(1)} %collective-permute-done, bf16[64,8192]{1,0:T(8,128)(2,1)S(1)} %collective-permute-done.1), kind=kOutput, calls=%fused_computation.1 | convolution fusion | flops 2164260864 | bytes 34865152 | tf_op jit(solution)/shard_map/dot_general | solution.py:34
  133.2 32.7 %add_convert_fusion = bf16[2048,8192]{1,0:T(8,128)(2,1)} fusion(bf16[2048,8192]{1,0:T(8,128)(2,1)} %convolution_convert_fusion, bf16[2048,8192]{1,0:T(8,128)(2,1)} %convolution_convert_fusion.1), kind=kLoop, calls=%fused_computation | loop fusion | flops 67108864 | bytes 100663296 | tf_op jit(solution)/shard_map/convert.2
  165.9 23.3 %fusion.13 = (bf16[2048,4096]{1,0:T(8,128)(2,1)}, bf16[2048,4096]{1,0:T(8,128)(2,1)}) fusion(bf16[2048,8192]{1,0:T(8,128)(2,1)} %add_convert_fusion), kind=kLoop, calls=%fused_computation.31 | loop fusion | bytes 67108864 | tf_op jit(solution)/shard_map/slice | solution.py:103
  (15 shorter events, 1.1 us)
Async XLA Ops:
  0.6 41.9 %copy-start = (bf16[64,4096]{1,0:T(8,128)(2,1)S(1)}, bf16[64,4096]{1,0:T(8,128)(2,1)}, u32[]{:S(2)}) copy-start(bf16[64,4096]{1,0:T(8,128)(2,1)} %param.7) | copy-start | bytes 1572868
  4.4 21.7 %all-to-all-start = ((bf16[16,4,4096]{2,1,0:T(4,128)(2,1)}), bf16[16,4,4096]{2,1,0:T(4,128)(2,1)S(1)}, u32[]{:S(2)}, u32[]{:S(2)}) async-start(bf16[16,4,4096]{2,1,0:T(4,128)(2,1)} %bitcast.1), calls=%async_computation | async-start | bytes 1048576 | tf_op jit(solution)/shard_map/all_to_all | solution.py:57
  26.9 82.8 %collective-permute-start = (bf16[64,2048]{1,0:T(8,128)(2,1)}, bf16[64,2048]{1,0:T(8,128)(2,1)S(1)}, u32[]{:S(2)}, u32[]{:S(2)}) collective-permute-start(bf16[64,2048]{1,0:T(8,128)(2,1)} %constant_dynamic-slice_fusion), channel_id=1, source_target_pairs={{0,16},{16,0},{1,17},{17,1},{2,18},{18,2},{3,19},{19,3},{4,20},{20... | collective-permute-start | bytes 786440 | tf_op jit(solution)/shard_map/ppermute | solution.py:18
  89.7 18.4 %all-to-all-start.1 = ((bf16[16,4,4096]{2,1,0:T(4,128)(2,1)}), bf16[16,4,4096]{2,1,0:T(4,128)(2,1)S(1)}, u32[]{:S(2)}, u32[]{:S(2)}) async-start(bf16[16,4,4096]{2,1,0:T(4,128)(2,1)} %reshape.67), calls=%async_computation.1 | async-start | bytes 1048576 | tf_op jit(solution)/shard_map/all_to_all | solution.py:75
  93.9 25.7 %collective-permute-start.1 = (bf16[64,8192]{1,0:T(8,128)(2,1)}, bf16[64,8192]{1,0:T(8,128)(2,1)S(1)}, u32[]{:S(2)}, u32[]{:S(2)}) collective-permute-start(bf16[64,8192]{1,0:T(8,128)(2,1)} %pad_maximum_fusion), channel_id=1, source_target_pairs={{0,16},{16,0},{1,17},{17,1},{2,18},{18,2},{3,19},{19,3},{4,20},{20... | collective-permute-start | bytes 3145736 | tf_op jit(solution)/shard_map/ppermute | solution.py:18
where the time goes:
time: 190 us; the launch traced here: 189 us
  matrix products  87.7 us (46%)
  other arithmetic  35 us (18%)
  local copies, waits for them, and re-layouts  28.7 us (15%)
  waiting for transfers between devices  23.3 us (12%)
  starting transfers between devices  13.7 us (7%)
    another operation x1, other arithmetic  32.7 us
    dot_general x2, matrix products, contract_rows(): lax.dot_general(left_rows, right_rows, (((0,), (0,)), ((), ())), preferre...  27.2 us
    slice x1, local copies, waits for them, and re-layouts, per_device(): up_weight_grad = weight_sum[:, ffd_cols:].astype(jnp.bfloat16)  23.3 us
    dot_general x1, matrix products, per_device(): lax.dot_general(up_grad, up_weight, transposed, preferred_element_type=jn...  15.6 us
    dot_general x1, matrix products, per_device(): lax.dot_general(gate_grad, gate_weight, transposed, preferred_element_typ...  15.5 us
    dot_general x1, matrix products, per_device(): jnp.dot(expert_rows, gate_weight, preferred_element_type=jnp.float32)  14 us
    dot_general x1, matrix products, per_device(): up_pre = jnp.dot(expert_rows, up_weight, preferred_element_type=jnp.float32)  14 us
    all_to_all x1, waiting for transfers between devices, per_device(): lax.all_to_all(copies, 'expert', split_axis=0, concat_axis=0, tiled=True)  13.4 us
  transfers between devices with their start and end apart: 4, of which 3 were waited for; matrix products, arithmetic and copies ran while one was open for 41% of the time, Pallas kernels for 0%

commit v1 on v0

v1 whole, which is shorter than its diff:
```python
import functools

import jax
import jax.numpy as jnp
from jax import lax
from jax.experimental import pallas as pl
from jax.experimental.pallas import tpu as pltpu
from jax.sharding import PartitionSpec as P


EXPERTS = 8
TOP = 2
CAP = 4


def from_partner(block, axis, apart):
    count = lax.axis_size(axis)
    route = []
    for low in range(count):
        high = low | 1 << apart
        if high != low and high < count:
            route += [(low, high), (high, low)]
    return lax.ppermute(block, axis, route)


def slot_tables(routing_dev):
    flat_experts = routing_dev.reshape(-1)
    onehot = (flat_experts[:, None] == jnp.arange(EXPERTS, dtype=jnp.int32)[None, :]).astype(
        jnp.int32
    )
    before = jnp.cumsum(onehot, axis=0) - onehot
    slot_index = jnp.sum(before * onehot, axis=1)
    target = flat_experts * CAP + slot_index
    placed = target[:, None] == jnp.arange(EXPERTS * CAP, dtype=jnp.int32)[None, :]
    return placed.astype(jnp.float32)


PIECES = 2
BLOCK = 512
WEIGHT_BLOCK = 256
TRANSPOSED = (((1,), (1,)), ((), ()))


def hidden_kernel(steps, first, *refs):
    if first:
        rows_ref, h_ref, gate_ref, up_ref, grads_ref, out_ref, total_ref = refs
    else:
        rows_ref, h_ref, gate_ref, up_ref, before_ref, grads_ref, out_ref, total_ref = refs
    step = pl.program_id(0)

    @pl.when(step == 0)
    def _():
        total_ref[...] = jnp.zeros_like(total_ref) if first else before_ref[...]

    rows = rows_ref[...]
    gate_pre = jnp.dot(rows, gate_ref[...], preferred_element_type=jnp.float32)
    up_pre = jnp.dot(rows, up_ref[...], preferred_element_type=jnp.float32)
    grad_h = h_ref[...].astype(jnp.float32)
    sig = jax.nn.sigmoid(gate_pre)
    gate_grad = (grad_h * up_pre * sig * (1.0 + gate_pre * (1.0 - sig))).astype(jnp.bfloat16)
    up_grad = (grad_h * gate_pre * sig).astype(jnp.bfloat16)
    grads_ref[0] = gate_grad
    grads_ref[1] = up_grad
    back = lax.dot_general(
        gate_grad, gate_ref[...], TRANSPOSED, preferred_element_type=jnp.float32
    ) + lax.dot_general(up_grad, up_ref[...], TRANSPOSED, preferred_element_type=jnp.float32)
    total_ref[...] += back

    @pl.when(step == steps - 1)
    def _():
        out_ref[...] = total_ref[...].astype(out_ref.dtype)


def hidden_pass(piece, pieces, block, rows, hidden, gate_weight, up_weight, before):
    count, width = rows.shape
    span = gate_weight.shape[1] // pieces
    steps = span // block
    first, last = piece == 0, piece == pieces - 1
    offset = piece * steps
    whole = pl.BlockSpec((count, width), lambda j: (0, 0))
    in_specs = [
        whole,
        pl.BlockSpec((count, block), lambda j: (0, offset + j)),
        pl.BlockSpec((width, block), lambda j: (0, offset + j)),
        pl.BlockSpec((width, block), lambda j: (0, offset + j)),
    ]
    args = [rows, hidden, gate_weight, up_weight]
    if not first:
        in_specs.append(whole)
        args.append(before)
    return pl.pallas_call(
        functools.partial(hidden_kernel, steps, first),
        grid=(steps,),
        in_specs=in_specs,
        out_specs=[pl.BlockSpec((2, count, block), lambda j: (0, 0, j)), whole],
        out_shape=[
            jax.ShapeDtypeStruct((2, count, span), jnp.bfloat16),
            jax.ShapeDtypeStruct((count, width), jnp.bfloat16 if last else jnp.float32),
        ],
        scratch_shapes=[pltpu.VMEM((count, width), jnp.float32)],
        cost_estimate=pl.CostEstimate(
            flops=8 * count * width * span,
            bytes_accessed=4 * width * span,
            transcendentals=count * span,
        ),
        compiler_params=pltpu.CompilerParams(
            dimension_semantics=("arbitrary",), vmem_limit_bytes=40 * 1024 * 1024
        ),
    )(*args)


def weight_kernel(*refs):
    own_ref, their_ref, own_grads, their_grads = refs[:4]
    gate_ref, up_ref, turned_ref = refs[-3:]

    @pl.when(pl.program_id(0) == 0)
    def _():
        both = jnp.concatenate([own_ref[...], their_ref[...]], axis=0)
        turned_ref[...] = both.T

    for at, out_ref in ((0, gate_ref), (1, up_ref)):
        grads = jnp.concatenate([own_grads[at], their_grads[at]], axis=0)
        out_ref[...] = jnp.dot(
            turned_ref[...], grads, preferred_element_type=jnp.float32
        ).astype(out_ref.dtype)


def weight_pass(piece, pieces, block, own, their, own_grads, their_grads, before):
    count, half = own.shape
    span = own_grads.shape[2]
    steps = span // block
    offset = piece * steps
    columns = pl.BlockSpec((count, half), lambda j: (0, 0))
    grads = pl.BlockSpec((2, count, block), lambda j: (0, 0, j))
    in_specs = [columns, columns, grads, grads]
    args = [own, their, own_grads, their_grads]
    aliases = {}
    if before is not None:
        in_specs += [pl.BlockSpec(memory_space=pl.ANY)] * 2
        args += list(before)
        aliases = {4: 0, 5: 1}
    result = jax.ShapeDtypeStruct((half, span * pieces), jnp.bfloat16)
    out = pl.BlockSpec((half, block), lambda j: (0, offset + j))
    return pl.pallas_call(
        weight_kernel,
        grid=(steps,),
        in_specs=in_specs,
        out_specs=[out, out],
        out_shape=[result, result],
        scratch_shapes=[pltpu.VMEM((half, 2 * count), jnp.bfloat16)],
        input_output_aliases=aliases,
        cost_estimate=pl.CostEstimate(
            flops=8 * count * half * span,
            bytes_accessed=4 * half * span,
            transcendentals=0,
        ),
        compiler_params=pltpu.CompilerParams(
            dimension_semantics=("arbitrary",), vmem_limit_bytes=40 * 1024 * 1024
        ),
    )(*args)


def layer(tokens, routing, hidden_grad, gate_weight, up_weight):
    token_count = tokens.shape[0]
    model_width = tokens.shape[1]
    ffd_cols = gate_weight.shape[1]
    shards = lax.axis_size("expert") // EXPERTS
    placed = slot_tables(routing)
    doubled = jnp.repeat(tokens, TOP, axis=0)
    outgoing = jnp.dot(
        placed.T.astype(jnp.bfloat16), doubled, preferred_element_type=jnp.float32
    ).astype(jnp.bfloat16)
    copies = jnp.broadcast_to(
        outgoing.reshape(EXPERTS, 1, CAP, model_width), (EXPERTS, shards, CAP, model_width)
    )
    copies = copies.reshape(EXPERTS * shards, CAP, model_width)
    arrived = lax.all_to_all(copies, "expert", split_axis=0, concat_axis=0, tiled=True)
    expert_rows = arrived.reshape(-1, model_width)
    half_width = model_width // lax.axis_size("dp")
    replica_index = lax.axis_index("dp")
    own_columns = lax.dynamic_slice_in_dim(expert_rows, replica_index * half_width, half_width, 1)
    far_columns = lax.dynamic_slice_in_dim(
        expert_rows, (1 - replica_index) * half_width, half_width, 1
    )
    their_columns = from_partner(far_columns, "dp", 0)
    pieces = PIECES
    block = min(BLOCK, ffd_cols // pieces)
    weight_block = min(WEIGHT_BLOCK, ffd_cols // pieces)
    partial_value = None
    pairs = []
    for piece in range(pieces):
        grads, partial_value = hidden_pass(
            piece, pieces, block, expert_rows, hidden_grad, gate_weight, up_weight, partial_value
        )
        pairs.append((grads, from_partner(grads, "dp", 0)))
    returned = lax.all_to_all(
        partial_value.reshape(-1, CAP, model_width),
        "expert",
        split_axis=0,
        concat_axis=0,
        tiled=True,
    )
    summed = jnp.sum(
        returned.astype(jnp.float32).reshape(EXPERTS, shards, CAP, model_width), axis=1
    )
    summed = summed.reshape(EXPERTS * CAP, model_width)
    gathered = jnp.dot(placed, summed, precision=lax.Precision.HIGHEST)
    token_grad = jnp.sum(gathered.reshape(token_count, TOP, model_width), axis=1).astype(
        jnp.bfloat16
    )
    weight_grads = None
    for piece, (own_grads, their_grads) in enumerate(pairs):
        weight_grads = weight_pass(
            piece, pieces, weight_block, own_columns, their_columns, own_grads, their_grads,
            weight_grads,
        )
    gate_weight_grad, up_weight_grad = weight_grads
    return (token_grad, gate_weight_grad, up_weight_grad)


def solution(mesh):
    in_specs = (
        P(("dp", "expert"), None),
        P(("dp", "expert"), None),
        P(("dp", "expert"), None),
        P(None, "expert"),
        P(None, "expert"),
    )
    out_specs = (P(("dp", "expert"), None), P("dp", "expert"), P("dp", "expert"))
    return jax.shard_map(layer, mesh=mesh, in_specs=in_specs, out_specs=out_specs, check_vma=False)
```

time: 190 us -> 123 us (0.65)
  matrix products: 87.7 us -> 1.31 us
  Pallas kernels: 0 us -> 58.2 us
  other arithmetic: 35 us -> 0.62 us
  local copies, waits for them, and re-layouts: 28.7 us -> 5.58 us
  blocking collectives: 0 us -> 21.5 us
  starting transfers between devices: 13.7 us -> 7.77 us
  waiting for transfers between devices: 23.3 us -> 26.6 us
    dot_general x8 -> x2, matrix products: 87.7 us -> 1.31 us  [the longest x1 1.11 us: layer(): gathered = jnp.dot(placed, summed, precision=lax.Precision.HIGHEST)]
    pallas_call x0 -> x4, Pallas kernels: none -> 58.2 us  [the longest x2 40.3 us: hidden_pass(): pl.pallas_call(functools.partial(hidden_kernel, steps, first), grid=(step...]
    another operation x1 -> x0, other arithmetic: 32.7 us -> none
    slice x1 -> x0, local copies, waits for them, and re-layouts: 23.3 us -> none  [per_device(): up_weight_grad = weight_sum[:, ffd_cols:].astype(jnp.bfloat16)]
    all_to_all x0 -> x1, blocking collectives: none -> 21.5 us  [layer(): lax.all_to_all(copies, 'expert', split_axis=0, concat_axis=0, tiled=True)]
    ppermute x2 -> x3, waiting for transfers between devices: 9.87 us -> 26.6 us  [from_partner(): return lax.ppermute(block, axis, route)]
    all_to_all x2 -> x1, waiting for transfers between devices: 13.5 us -> 0.01 us  [layer(): lax.all_to_all(partial_value.reshape(-1, CAP, model_width), 'expert', spl...]
    all_to_all x2 -> x1, starting transfers between devices: 11.6 us -> 4.16 us  [layer(): lax.all_to_all(partial_value.reshape(-1, CAP, model_width), 'expert', spl...]
  transfers between devices with their start and end apart: 4 -> 4, of which waited for: 3 -> 1; matrix products, arithmetic and copies ran while one was open for 41% -> 1% of each run, Pallas kernels for 0% -> 15%
where the time goes in v1:
time: 123 us; the launch traced here: 122 us
  Pallas kernels  58.2 us (47%)
  waiting for transfers between devices  26.6 us (22%)
  blocking collectives  21.5 us (17%)
  starting transfers between devices  7.77 us (6%)
  local copies, waits for them, and re-layouts  5.58 us (5%)
  matrix products  1.31 us (1%)
    pallas_call x2, Pallas kernels, hidden_pass(): pl.pallas_call(functools.partial(hidden_kernel, steps, first), grid=(step...  40.3 us
    ppermute x3, waiting for transfers between devices, from_partner(): return lax.ppermute(block, axis, route)  26.6 us
    all_to_all x1, blocking collectives, layer(): lax.all_to_all(copies, 'expert', split_axis=0, concat_axis=0, tiled=True)  21.5 us
    pallas_call x2, Pallas kernels, weight_pass(): pl.pallas_call(weight_kernel, grid=(steps,), in_specs=in_specs, out_specs...  17.9 us
    all_to_all x1, starting transfers between devices, layer(): lax.all_to_all(partial_value.reshape(-1, CAP, model_width), 'expert', spl...  4.16 us
    ppermute x3, starting transfers between devices, from_partner(): return lax.ppermute(block, axis, route)  3.61 us
  transfers between devices with their start and end apart: 4, of which 1 were waited for; matrix products, arithmetic and copies ran while one was open for 1% of the time, Pallas kernels for 15%

profile of v1, /device:TPU:0, one launch (start us, length us, event | category | flops | bytes accessed | tf_op | source)
XLA Modules:
  0.0 122.3 jit_solution(5218655624832717060)
XLA Ops:
  0.6 0.8 copy.18
  1.6 0.2 select_reduce_fusion
  1.8 1.1 broadcast_in_dim.6
  2.9 0.1 reshape.64
  3.0 0.2 convolution_convert_fusion
  3.2 0.1 broadcast_in_dim.14
  3.3 0.2 broadcast_in_dim.15
  3.6 21.5 %all_to_all.10 = bf16[16,4,4096]{2,1,0:T(4,128)(2,1)S(1)} all-to-all(bf16[16,4,4096]{2,1,0:T(4,128)(2,1)S(1)} %bitcast.9), channel_id=1, replica_groups=mesh['dp'=2,'expert'=16] {'expert'}, dimensions={0} | all-to-all | bytes 1048576 | tf_op jit(solution)/shard_map/all_to_all | solution.py:177
  25.0 0.1 reshape.66.refs_0_
  25.1 1.0 copy-done
  26.2 20.1 %shard_map.76 = (bf16[2,64,2048]{2,1,0:T(8,128)(2,1)S(1)}, f32[64,4096]{1,0:T(8,128)S(1)}) custom-call(bf16[64,4096]{1,0:T(8,128)(2,1)S(1)} %reshape.66.refs_0_, bf16[64,4096]{1,0:T(8,128)(2,1)S(1)} %copy-done, bf16[4096,4096]{1,0:T(8,128)(2,1)} %refs_2_.3, bf16[4096,4096]{1,0:T(8,128)(2,1)} %refs_3_.3), custom_call_target="tpu_custom_call" | custom-call | flops 4294967296 | bytes 33554432 | tf_op jit(solution)/shard_map/pallas_call | solution.py:91
  46.3 20.2 %shard_map.77 = (bf16[2,64,2048]{2,1,0:T(8,128)(2,1)S(1)}, bf16[64,4096]{1,0:T(8,128)(2,1)S(1)}) custom-call(bf16[64,4096]{1,0:T(8,128)(2,1)S(1)} %reshape.66.refs_0_, bf16[64,4096]{1,0:T(8,128)(2,1)S(1)} %copy-done, bf16[4096,4096]{1,0:T(8,128)(2,1)} %refs_2_.3, bf16[4096,4096]{1,0:T(8,128)(2,1)} %refs_3_.3, f32[64,4096]{1,0:T(8,128)S(1)} %get-tuple-element.11.refs_4_), custom_call_target="tpu_custom_call" | custom-call | flops 4294967296 | bytes 33554432 | tf_op jit(solution)/shard_map/pallas_call | solution.py:91
  66.5 1.0 reshape.67
  67.5 4.2 %all-to-all-start.1 = ((bf16[16,4,4096]{2,1,0:T(4,128)(2,1)}), bf16[16,4,4096]{2,1,0:T(4,128)(2,1)S(1)}, u32[]{:S(2)}, u32[]{:S(2)}) async-start(bf16[16,4,4096]{2,1,0:T(4,128)(2,1)} %reshape.67), calls=%async_computation.1 | async-start | bytes 1048576 | tf_op jit(solution)/shard_map/all_to_all | solution.py:196
  71.7 1.6 %collective-permute-start.2 = (bf16[2,64,2048]{2,1,0:T(8,128)(2,1)S(1)}, bf16[2,64,2048]{2,1,0:T(8,128)(2,1)S(1)}, u32[]{:S(2)}, u32[]{:S(2)}) collective-permute-start(bf16[2,64,2048]{2,1,0:T(8,128)(2,1)S(1)} %get-tuple-element.14.refs_2_), channel_id=1, source_target_pairs={{0,16},{16,0},{1,17},{17,1},{2,18},{18,2},{3,19},{19,3},{4,20},{20... | collective-permute-start | bytes 1572872 | tf_op jit(solution)/shard_map/ppermute | solution.py:23
  73.3 0.5 collective-permute-start.1
  73.8 0.7 constant_dynamic-slice_fusion.1
  74.5 1.5 %collective-permute-start = (bf16[64,2048]{1,0:T(8,128)(2,1)}, bf16[64,2048]{1,0:T(8,128)(2,1)S(1)}, u32[]{:S(2)}, u32[]{:S(2)}) collective-permute-start(bf16[64,2048]{1,0:T(8,128)(2,1)} %get-tuple-element.19), channel_id=1, source_target_pairs={{0,16},{16,0},{1,17},{17,1},{2,18},{18,2},{3,19},{19,3},{4,20},{20... | collective-permute-start | bytes 786440 | tf_op jit(solution)/shard_map/ppermute | solution.py:23
  76.2 26.6 %collective-permute-done.refs_1_ = bf16[64,2048]{1,0:T(8,128)(2,1)S(1)} collective-permute-done((bf16[64,2048]{1,0:T(8,128)(2,1)}, bf16[64,2048]{1,0:T(8,128)(2,1)S(1)}, u32[]{:S(2)}, u32[]{:S(2)}) %collective-permute-start) | collective-permute-done | bytes 262176 | tf_op jit(solution)/shard_map/ppermute | solution.py:23
  102.8 9.0 %shard_map.78 = (bf16[2048,4096]{1,0:T(8,128)(2,1)}, bf16[2048,4096]{1,0:T(8,128)(2,1)}) custom-call(bf16[64,2048]{1,0:T(8,128)(2,1)S(1)} %get-tuple-element.20.refs_0_, bf16[64,2048]{1,0:T(8,128)(2,1)S(1)} %collective-permute-done.refs_1_, bf16[2,64,2048]{2,1,0:T(8,128)(2,1)S(1)} %get-tuple-element.14.refs_2_, ...), custom_call_target="tpu_custom_call" | custom-call | flops 2147483648 | bytes 16777216 | tf_op jit(solution)/shard_map/pallas_call | solution.py:144
  111.7 9.0 %shard_map.79 = (bf16[2048,4096]{1,0:T(8,128)(2,1)}, bf16[2048,4096]{1,0:T(8,128)(2,1)}) custom-call(bf16[64,2048]{1,0:T(8,128)(2,1)S(1)} %get-tuple-element.20.refs_0_, bf16[64,2048]{1,0:T(8,128)(2,1)S(1)} %collective-permute-done.refs_1_, bf16[2,64,2048]{2,1,0:T(8,128)(2,1)S(1)} %get-tuple-element.13.refs_2_, ...), custom_call_target="tpu_custom_call", output_to_operand_aliasing={{0}: (4, {}), {1}: (5, {})} | custom-call | flops 2147483648 | bytes 16777216 | tf_op jit(solution)/shard_map/pallas_call | solution.py:144
  120.7 0.3 convert_reduce_fusion
  121.0 0.2 reshape.73
  121.2 1.1 convolution_reduce_fusion
  (13 shorter events, 0.4 us)
Async XLA Ops:
  25.1 1.0 copy-start
  46.3 29.9 %copy-start.1 = (s32[16,2]{0,1:T(2,128)S(1)}, s32[16,2]{0,1:T(2,128)}, u32[]{:S(2)}) copy-start(s32[16,2]{0,1:T(2,128)} %param.6) | copy-start | bytes 388
  67.5 53.2 %all-to-all-start.1 = ((bf16[16,4,4096]{2,1,0:T(4,128)(2,1)}), bf16[16,4,4096]{2,1,0:T(4,128)(2,1)S(1)}, u32[]{:S(2)}, u32[]{:S(2)}) async-start(bf16[16,4,4096]{2,1,0:T(4,128)(2,1)} %reshape.67), calls=%async_computation.1 | async-start | bytes 1048576 | tf_op jit(solution)/shard_map/all_to_all | solution.py:196
  71.7 31.1 %collective-permute-start.2 = (bf16[2,64,2048]{2,1,0:T(8,128)(2,1)S(1)}, bf16[2,64,2048]{2,1,0:T(8,128)(2,1)S(1)}, u32[]{:S(2)}, u32[]{:S(2)}) collective-permute-start(bf16[2,64,2048]{2,1,0:T(8,128)(2,1)S(1)} %get-tuple-element.14.refs_2_), channel_id=1, source_target_pairs={{0,16},{16,0},{1,17},{17,1},{2,18},{18,2},{3,19},{19,3},{4,20},{20... | collective-permute-start | bytes 1572872 | tf_op jit(solution)/shard_map/ppermute | solution.py:23
  73.3 38.5 %collective-permute-start.1 = (bf16[2,64,2048]{2,1,0:T(8,128)(2,1)S(1)}, bf16[2,64,2048]{2,1,0:T(8,128)(2,1)S(1)}, u32[]{:S(2)}, u32[]{:S(2)}) collective-permute-start(bf16[2,64,2048]{2,1,0:T(8,128)(2,1)S(1)} %get-tuple-element.13.refs_2_), channel_id=1, source_target_pairs={{0,16},{16,0},{1,17},{17,1},{2,18},{18,2},{3,19},{19,3},{4,20},{20... | collective-permute-start | bytes 1572872 | tf_op jit(solution)/shard_map/ppermute | solution.py:23
  74.5 28.3 %collective-permute-start = (bf16[64,2048]{1,0:T(8,128)(2,1)}, bf16[64,2048]{1,0:T(8,128)(2,1)S(1)}, u32[]{:S(2)}, u32[]{:S(2)}) collective-permute-start(bf16[64,2048]{1,0:T(8,128)(2,1)} %get-tuple-element.19), channel_id=1, source_target_pairs={{0,16},{16,0},{1,17},{17,1},{2,18},{18,2},{3,19},{19,3},{4,20},{20... | collective-permute-start | bytes 786440 | tf_op jit(solution)/shard_map/ppermute | solution.py:23
